TPU v7x, 128 devices: a whole 4x4x4 slice. The times are simulated.
128 devices in a mesh: date: 16 (over y, x), pix: 4 (over z), tile: 2 (over core).
Axes of the slice: x: 4, y: 4, z: 4, core: 2. Of those that a mesh axis runs over, the one named last changes fastest.
Arguments:
- reflectance: float32 [128, 7, 65536], P('date', None, ('tile', 'pix')), parts along dimension 2, may hold values from -6 to 6
- validity: int32 [128, 65536], P('date', ('tile', 'pix')), parts along dimension 1, may hold values from 0 to 1, as said below
- day_number: int32 [128], P('date'), may hold values from 1 to 255, as said below
Outputs:
- filled: float32 [128, 7, 65536], P('date', None, ('tile', 'pix')), parts along dimension 2
There are 2 independent parts, one for each index of `tile`. A program takes and returns all parts, laid end to end along the dimension named above; an argument that names none is the same for every part. Nothing has to cross between parts.
Inputs may be any that keep to these rules, and one draw needn't show every extreme that they name: `validity`: 1 marks a usable observation, 0 a rejected one. `day_number`: strictly increasing along the dates, by 1 to 3 days from one date to the next, starting at day 1.
All inputs are finite; a program needn't handle non-finite values.
Results may differ from a plain program's by a relative error of at most 0.0003.
Values sent between devices are 32-bit elements; how exact they have to be, the bound alone decides.
A program may use at most 64 MiB of HBM per device.

v0:
```python
import jax
import jax.numpy as jnp
from jax import lax
from jax.sharding import Mesh
from jax.sharding import PartitionSpec as P

DATE = ("date_0", "date_1")


far_day = 1073741824


def nothing_yet(array, identity):
    return jax.tree.map(
        lambda part, zero: jnp.zeros_like(part) + jnp.asarray(zero, part.dtype), array, identity
    )


def entering(array, axes, combine, identity, reverse):
    before = start = nothing_yet(array, identity)
    subtotal = array
    for axis in reversed(axes):
        size, mine = (lax.axis_size(axis), lax.axis_index(axis))
        pieces = jax.tree.map(lambda part: lax.all_gather(part, axis), subtotal)
        inside, subtotal = (start, start)
        for k in reversed(range(size)) if reverse else range(size):
            passed = k > mine if reverse else k < mine
            subtotal = combine(subtotal, jax.tree.map(lambda part: part[k], pieces))
            inside = jax.tree.map(lambda new, old: jnp.where(passed, new, old), subtotal, inside)
        before = combine(inside, before)
    return before


def pass_forward(earlier, later):
    keep = later[0] >= 0
    return (
        jnp.where(keep, later[0], earlier[0]),
        jnp.where(keep[:, None, :], later[1], earlier[1]),
    )


def pass_backward(earlier, later):
    keep = later[0] < far_day
    return (
        jnp.where(keep, later[0], earlier[0]),
        jnp.where(keep[:, None, :], later[1], earlier[1]),
    )


def scan_block(values, validity, days):
    live = validity > 0
    day_col = jnp.broadcast_to(days[:, None], validity.shape)
    fwd_day, fwd_val = lax.associative_scan(
        pass_forward, (jnp.where(live, day_col, -1), values), axis=0
    )
    bwd_day, bwd_val = lax.associative_scan(
        pass_backward, (jnp.where(live, day_col, far_day), values), reverse=True, axis=0
    )
    return (live, day_col, fwd_day, fwd_val, bwd_day, bwd_val)


def blend(values, live, day_col, fwd_day, fwd_val, bwd_day, bwd_val):
    has_prev = fwd_day >= 0
    has_next = bwd_day < far_day
    inside = has_prev & has_next & jnp.logical_not(live)
    span = jnp.where(inside, bwd_day - fwd_day, 1).astype(jnp.float32)
    weight = (day_col - fwd_day).astype(jnp.float32) / span
    middle = fwd_val + weight[:, None, :] * (bwd_val - fwd_val)
    one_side = jnp.where(
        has_prev[:, None, :],
        fwd_val,
        jnp.where(has_next[:, None, :], bwd_val, jnp.zeros_like(fwd_val)),
    )
    chosen = jnp.where(inside[:, None, :], middle, one_side)
    return jnp.where(live[:, None, :], values, chosen)


def take_forward(earlier, later):
    keep = later[0] >= 0
    return (jnp.where(keep, later[0], earlier[0]), jnp.where(keep[None], later[1], earlier[1]))


def take_backward(earlier, later):
    keep = later[0] < far_day
    return (jnp.where(keep, later[0], earlier[0]), jnp.where(keep[None], later[1], earlier[1]))


def body(reflectance, validity, day_number):
    live, day_col, fwd_day, fwd_val, bwd_day, bwd_val = scan_block(
        reflectance, validity, day_number
    )
    pixels = reflectance.shape[2]
    bands = reflectance.shape[1]
    none_before = jnp.full((pixels,), -1, jnp.int32)
    none_after = jnp.full((pixels,), far_day, jnp.int32)
    blank = jnp.zeros((bands, pixels), jnp.float32)
    in_fday, in_fval = entering(
        (fwd_day[-1], fwd_val[-1]), DATE, take_forward, (none_before, blank), False
    )
    in_bday, in_bval = entering(
        (bwd_day[0], bwd_val[0]), DATE, take_backward, (none_after, blank), True
    )
    keep_f = fwd_day >= 0
    fwd_day = jnp.where(keep_f, fwd_day, in_fday[None])
    fwd_val = jnp.where(keep_f[:, None, :], fwd_val, in_fval[None])
    keep_b = bwd_day < far_day
    bwd_day = jnp.where(keep_b, bwd_day, in_bday[None])
    bwd_val = jnp.where(keep_b[:, None, :], bwd_val, in_bval[None])
    return blend(reflectance, live, day_col, fwd_day, fwd_val, bwd_day, bwd_val)


def solution(mesh):
    torus = Mesh(
        mesh.devices.reshape(4, 4, mesh.shape["pix"], mesh.shape["tile"]),
        ("date_0", "date_1", "pix", "tile"),
    )
    placed = (P(DATE, None, ("tile", "pix")), P(DATE, ("tile", "pix")), P(DATE))
    return jax.shard_map(
        body, mesh=torus, in_specs=placed, out_specs=P(DATE, None, ("tile", "pix")), check_vma=False
    )
```

profile of v0, /device:TPU:0, one launch (start us, length us, event | category | flops | bytes accessed | tf_op | source)
XLA Modules:
  0.0 171.1 jit_solution(10882193708447139703)
XLA Ops:
  0.0 1.1 broadcast_select_fusion.2
  6.2 12.5 %all-gather = s32[4,1,8192]{2,1,0:T(1,128)S(1)} all-gather(s32[1,1,8192]{2,1,0:T(1,128)S(1)} %add_bitcast_fusion.1), channel_id=1, replica_groups=mesh['date_0'=4,'date_1'=4,'pix'=4,'tile'=2] {'date_1'}, dimensions={0}, use_global_device_ids=true | all-gather | bytes 163840 | tf_op jit(solution)/shard_map/all_gather | solution.py:24
  18.6 1.1 compare_reduce_fusion.17
  19.8 12.5 %all-gather.1 = s32[4,1,8192]{2,1,0:T(1,128)S(1)} all-gather(s32[1,1,8192]{2,1,0:T(1,128)S(1)} %bitcast.169), channel_id=1, replica_groups=mesh['date_0'=4,'date_1'=4,'pix'=4,'tile'=2] {'date_0'}, dimensions={0}, use_global_device_ids=true | all-gather | bytes 163840 | tf_op jit(solution)/shard_map/all_gather | solution.py:24
  32.4 1.0 compare_reduce_fusion.14
  34.4 1.6 slice.313
  37.5 1.6 slice.309
  39.1 1.6 slice.311
  45.4 12.0 %all-gather.2 = s32[4,1,8192]{2,1,0:T(1,128)S(1)} all-gather(s32[1,1,8192]{2,1,0:T(1,128)S(1)} %add_bitcast_fusion), channel_id=1, replica_groups=mesh['date_0'=4,'date_1'=4,'pix'=4,'tile'=2] {'date_1'}, dimensions={0}, use_global_device_ids=true | all-gather | bytes 163840 | tf_op jit(solution)/shard_map/all_gather | solution.py:24
  57.5 1.0 compare_reduce_fusion.6
  58.5 12.2 %all-gather.3 = s32[4,1,8192]{2,1,0:T(1,128)S(1)} all-gather(s32[1,1,8192]{2,1,0:T(1,128)S(1)} %fusion.23), channel_id=1, replica_groups=mesh['date_0'=4,'date_1'=4,'pix'=4,'tile'=2] {'date_0'}, dimensions={0}, use_global_device_ids=true | all-gather | bytes 163840 | tf_op jit(solution)/shard_map/all_gather | solution.py:24
  70.9 1.0 compare_reduce_fusion.3
  73.6 2.6 %copy.18 = f32[8,7,8192]{2,1,0:T(8,128)S(1)} copy(f32[8,7,8192]{2,0,1:T(8,128)} %param.3) | data formatting | bytes 3670016 | tf_op args[0]
  81.4 1.1 pad.90
  82.5 2.7 %pad.91 = f32[4,7,8192]{2,1,0:T(8,128)} pad(f32[2,7,8192]{2,1,0:T(8,128)} %pad_add_fusion.1, f32[]{:T(128)} %constant.17.clone.1), padding=1_0_1x0_0_0x0_0_0 | pad | bytes 1376260 | tf_op jit(solution)/shard_map/pad | solution.py:53
  85.2 2.4 %add_select_fusion.1 = (f32[3,7,8192]{2,1,0:T(8,128)S(1)}, f32[3,7,8192]{2,1,0:T(8,128)}) fusion(f32[4,7,8192]{2,1,0:T(8,128)} %pad.91, f32[4,7,8192]{2,1,0:T(8,128)S(1)} %pad.90, f32[8,7,8192]{2,1,0:T(8,128)S(1)} %copy.18, pred[3,8192]{1,0:T(4,128)(4,1)S(1)} %broadcast_compare_fusion.6), kind=kLoop, calls=%fused_computation.5 | loop fusion | flops 344064 | bytes 4153344 | tf_op jit(solution)/shard_map/jit(_where)/select_n | solution.py:38
  87.6 1.1 add.94
  88.7 1.1 pad_maximum_fusion
  92.9 1.1 pad_maximum_fusion.1
  94.0 2.2 %pad.98 = f32[8,7,8192]{2,1,0:T(8,128)S(1)} pad(f32[4,7,8192]{2,1,0:T(8,128)} %pad_maximum_fusion.1, f32[]{:T(128)} %constant.17.clone.1), padding=0_1_1x0_0_0x0_0_0 | pad | bytes 2752516 | tf_op jit(solution)/shard_map/pad | solution.py:56
  96.2 2.9 %pad.99 = f32[8,7,8192]{2,1,0:T(8,128)} pad(f32[4,7,8192]{2,1,0:T(8,128)S(1)} %add.97, f32[]{:T(128)} %constant.17.clone.1), padding=1_0_1x0_0_0x0_0_0 | pad | bytes 2752516 | tf_op jit(solution)/shard_map/pad | solution.py:56
  99.0 1.0 slice_add_fusion
  100.0 3.2 %add.98 = f32[8,7,8192]{2,1,0:T(8,128)} add(f32[8,7,8192]{2,1,0:T(8,128)S(1)} %pad.98, f32[8,7,8192]{2,1,0:T(8,128)} %pad.99) | non-fusion elementwise | flops 458752 | bytes 5505024 | tf_op jit(solution)/shard_map/add | solution.py:56
  103.2 14.0 %all_gather.34 = f32[4,7,8192]{2,1,0:T(8,128)S(1)} all-gather(f32[1,7,8192]{2,1,0:T(8,128)S(1)} %slice_add_fusion), channel_id=1, replica_groups=mesh['date_0'=4,'date_1'=4,'pix'=4,'tile'=2] {'date_1'}, dimensions={0}, use_global_device_ids=true | all-gather | bytes 1146880 | tf_op jit(solution)/shard_map/all_gather | solution.py:24
  117.3 13.8 %all_gather.35 = f32[4,7,8192]{2,1,0:T(8,128)S(1)} all-gather(f32[1,7,8192]{2,1,0:T(8,128)S(1)} %slice_select_fusion.9), channel_id=1, replica_groups=mesh['date_0'=4,'date_1'=4,'pix'=4,'tile'=2] {'date_0'}, dimensions={0}, use_global_device_ids=true | all-gather | bytes 1146880 | tf_op jit(solution)/shard_map/all_gather | solution.py:24
  131.6 2.3 %pad.92 = f32[8,7,8192]{2,1,0:T(8,128)S(1)} pad(f32[4,7,8192]{2,1,0:T(8,128)} %pad_maximum_fusion, f32[]{:T(128)} %constant.17.clone.1), padding=0_1_1x0_0_0x0_0_0 | pad | bytes 2752516 | tf_op jit(solution)/shard_map/pad | solution.py:53
  133.9 2.9 %pad.93 = f32[8,7,8192]{2,1,0:T(8,128)} pad(f32[4,7,8192]{2,1,0:T(8,128)S(1)} %copy-done.4, f32[]{:T(128)} %constant.17.clone.1), padding=1_0_1x0_0_0x0_0_0 | pad | bytes 2752516 | tf_op jit(solution)/shard_map/pad | solution.py:53
  136.8 1.0 slice_add_fusion.1
  137.9 14.0 %all_gather.32 = f32[4,7,8192]{2,1,0:T(8,128)S(1)} all-gather(f32[1,7,8192]{2,1,0:T(8,128)S(1)} %slice_add_fusion.1), channel_id=1, replica_groups=mesh['date_0'=4,'date_1'=4,'pix'=4,'tile'=2] {'date_1'}, dimensions={0}, use_global_device_ids=true | all-gather | bytes 1146880 | tf_op jit(solution)/shard_map/all_gather | solution.py:24
  152.1 14.0 %all_gather.33 = f32[4,7,8192]{2,1,0:T(8,128)S(1)} all-gather(f32[1,7,8192]{2,1,0:T(8,128)S(1)} %slice_select_fusion.18), channel_id=1, replica_groups=mesh['date_0'=4,'date_1'=4,'pix'=4,'tile'=2] {'date_0'}, dimensions={0}, use_global_device_ids=true | all-gather | bytes 1146880 | tf_op jit(solution)/shard_map/all_gather | solution.py:24
  166.5 2.3 %select_select_fusion = f32[8,7,8192]{2,1,0:T(8,128)S(1)} fusion(f32[8,7,8192]{2,1,0:T(8,128)S(1)} %copy-done.1, f32[8,7,8192]{2,1,0:T(8,128)S(1)} %pad.92, f32[8,7,8192]{2,1,0:T(8,128)S(1)} %copy-done, f32[7,8192]{1,0:T(8,128)S(1)} %fusion.6, f32[8,8192]{1,0:T(8,128)S(1)} %copy-done.8, f32[7,8192]{1,0:T(8,128)S(1)} %fusion.9, ...), kind=kLoop, calls=%fused_computation | loop fusion | flops 4587520 | bytes 10289152 | tf_op jit(solution)/shard_map/jit(_where)/select_n | solution.py:75
  168.8 2.3 %copy.19 = f32[8,7,8192]{2,0,1:T(8,128)} copy(f32[8,7,8192]{2,1,0:T(8,128)S(1)} %select_select_fusion) | data formatting | bytes 3670016 | tf_op jit(solution)/shard_map/jit(_where)/select_n | solution.py:75
  (145 shorter events, 23.5 us)
Async XLA Ops:
  5.4 28.0 %copy-start.31 = (s32[8]{0:T(128)S(1)}, s32[8]{0:T(128)}, u32[]{:S(2)}) copy-start(s32[8]{0:T(128)} %param.5) | copy-start | bytes 100
  85.2 2.4 %copy-start.2 = (f32[4,7,8192]{2,1,0:T(8,128)S(1)}, f32[4,7,8192]{2,1,0:T(8,128)}, u32[]{:S(2)}) copy-start(f32[4,7,8192]{2,1,0:T(8,128)} %pad.91) | copy-start | bytes 2752516
  87.6 1.1 copy-start.10
  87.6 2.3 %copy-start.7 = (f32[2,7,8192]{2,1,0:T(8,128)S(1)}, f32[2,7,8192]{2,1,0:T(8,128)}, u32[]{:S(2)}) copy-start(f32[2,7,8192]{2,1,0:T(8,128)} %pad_maximum_fusion.3) | copy-start | bytes 1376260
  88.7 1.3 copy-start.6
  89.9 1.1 copy-start.5
  92.0 1.0 copy-start.9
  100.0 17.2 %copy-start.15 = (pred[8192]{0:T(1024)(128)(4,1)S(1)}, pred[8192]{0:T(1024)(128)(4,1)}, u32[]{:S(2)}) copy-start(pred[8192]{0:T(1024)(128)(4,1)} %get-tuple-element.19) | copy-start | bytes 24580
  100.0 17.2 %copy-start.16 = (pred[8192]{0:T(1024)(128)(4,1)S(1)}, pred[8192]{0:T(1024)(128)(4,1)}, u32[]{:S(2)}) copy-start(pred[8192]{0:T(1024)(128)(4,1)} %get-tuple-element.20) | copy-start | bytes 24580
  103.2 28.0 %copy-start.25 = (pred[8192]{0:T(1024)(128)(4,1)S(1)}, pred[8192]{0:T(1024)(128)(4,1)}, u32[]{:S(2)}) copy-start(pred[8192]{0:T(1024)(128)(4,1)} %get-tuple-element.13) | copy-start | bytes 24580
  103.2 28.0 %copy-start.26 = (pred[8192]{0:T(1024)(128)(4,1)S(1)}, pred[8192]{0:T(1024)(128)(4,1)}, u32[]{:S(2)}) copy-start(pred[8192]{0:T(1024)(128)(4,1)} %get-tuple-element.14) | copy-start | bytes 24580
  103.2 28.0 %copy-start.27 = (pred[8192]{0:T(1024)(128)(4,1)S(1)}, pred[8192]{0:T(1024)(128)(4,1)}, u32[]{:S(2)}) copy-start(pred[8192]{0:T(1024)(128)(4,1)} %get-tuple-element.15) | copy-start | bytes 24580
  103.2 28.0 %copy-start.28 = (pred[8192]{0:T(1024)(128)(4,1)S(1)}, pred[8192]{0:T(1024)(128)(4,1)}, u32[]{:S(2)}) copy-start(pred[8192]{0:T(1024)(128)(4,1)} %get-tuple-element.16) | copy-start | bytes 24580
  103.2 28.0 %copy-start.29 = (pred[8192]{0:T(1024)(128)(4,1)S(1)}, pred[8192]{0:T(1024)(128)(4,1)}, u32[]{:S(2)}) copy-start(pred[8192]{0:T(1024)(128)(4,1)} %compare_reduce_fusion.4) | copy-start | bytes 24580
  131.6 2.3 %copy-start.4 = (f32[4,7,8192]{2,1,0:T(8,128)S(1)}, f32[4,7,8192]{2,1,0:T(8,128)}, u32[]{:S(2)}) copy-start(f32[4,7,8192]{2,1,0:T(8,128)} %add.94) | copy-start | bytes 2752516
  133.8 18.0 %copy-start.17 = (pred[8192]{0:T(1024)(128)(4,1)S(1)}, pred[8192]{0:T(1024)(128)(4,1)}, u32[]{:S(2)}) copy-start(pred[8192]{0:T(1024)(128)(4,1)} %get-tuple-element.9) | copy-start | bytes 24580
  133.9 18.0 %copy-start.18 = (pred[8192]{0:T(1024)(128)(4,1)S(1)}, pred[8192]{0:T(1024)(128)(4,1)}, u32[]{:S(2)}) copy-start(pred[8192]{0:T(1024)(128)(4,1)} %get-tuple-element.10) | copy-start | bytes 24580
  136.8 15.1 %copy-start.19 = (pred[8192]{0:T(1024)(128)(4,1)S(1)}, pred[8192]{0:T(1024)(128)(4,1)}, u32[]{:S(2)}) copy-start(pred[8192]{0:T(1024)(128)(4,1)} %get-tuple-element.11) | copy-start | bytes 24580
  136.8 15.1 %copy-start.20 = (pred[8192]{0:T(1024)(128)(4,1)S(1)}, pred[8192]{0:T(1024)(128)(4,1)}, u32[]{:S(2)}) copy-start(pred[8192]{0:T(1024)(128)(4,1)} %get-tuple-element.12) | copy-start | bytes 24580
  136.8 29.7 %copy-start.12 = (pred[8,8192]{1,0:T(8,128)(4,1)S(1)}, pred[8,8192]{1,0:T(8,128)(4,1)}, u32[]{:S(2)}) copy-start(pred[8,8192]{1,0:T(8,128)(4,1)} %get-tuple-element.25) | copy-start | bytes 196612
  136.8 29.7 %copy-start.13 = (pred[8,8192]{1,0:T(8,128)(4,1)S(1)}, pred[8,8192]{1,0:T(8,128)(4,1)}, u32[]{:S(2)}) copy-start(pred[8,8192]{1,0:T(8,128)(4,1)} %get-tuple-element.26) | copy-start | bytes 196612
  136.8 29.7 %copy-start.14 = (pred[8,8192]{1,0:T(8,128)(4,1)S(1)}, pred[8,8192]{1,0:T(8,128)(4,1)}, u32[]{:S(2)}) copy-start(pred[8,8192]{1,0:T(8,128)(4,1)} %get-tuple-element.27) | copy-start | bytes 196612
  137.8 28.2 %copy-start.21 = (pred[8192]{0:T(1024)(128)(4,1)S(1)}, pred[8192]{0:T(1024)(128)(4,1)}, u32[]{:S(2)}) copy-start(pred[8192]{0:T(1024)(128)(4,1)} %get-tuple-element.5) | copy-start | bytes 24580
  137.9 28.2 %copy-start.22 = (pred[8192]{0:T(1024)(128)(4,1)S(1)}, pred[8192]{0:T(1024)(128)(4,1)}, u32[]{:S(2)}) copy-start(pred[8192]{0:T(1024)(128)(4,1)} %get-tuple-element.6) | copy-start | bytes 24580
  137.9 28.2 %copy-start.23 = (pred[8192]{0:T(1024)(128)(4,1)S(1)}, pred[8192]{0:T(1024)(128)(4,1)}, u32[]{:S(2)}) copy-start(pred[8192]{0:T(1024)(128)(4,1)} %get-tuple-element.7) | copy-start | bytes 24580
  137.9 28.2 %copy-start.24 = (pred[8192]{0:T(1024)(128)(4,1)S(1)}, pred[8192]{0:T(1024)(128)(4,1)}, u32[]{:S(2)}) copy-start(pred[8192]{0:T(1024)(128)(4,1)} %get-tuple-element.8) | copy-start | bytes 24580
  137.9 28.2 %copy-start.30 = (pred[8192]{0:T(1024)(128)(4,1)S(1)}, pred[8192]{0:T(1024)(128)(4,1)}, u32[]{:S(2)}) copy-start(pred[8192]{0:T(1024)(128)(4,1)} %get-tuple-element.47) | copy-start | bytes 24580
  137.9 28.6 %copy-start.3 = (f32[8,7,8192]{2,0,1:T(8,128)S(1)}, f32[8,7,8192]{2,0,1:T(8,128)}, u32[]{:S(2)}) copy-start(f32[8,7,8192]{2,0,1:T(8,128)} %param.3) | copy-start | bytes 5505028
  151.9 14.6 %copy-start.1 = (f32[8,7,8192]{2,1,0:T(8,128)S(1)}, f32[8,7,8192]{2,1,0:T(8,128)}, u32[]{:S(2)}) copy-start(f32[8,7,8192]{2,1,0:T(8,128)} %add.98) | copy-start | bytes 5505028
  152.1 14.5 %copy-start = (f32[8,7,8192]{2,1,0:T(8,128)S(1)}, f32[8,7,8192]{2,1,0:T(8,128)}, u32[]{:S(2)}) copy-start(f32[8,7,8192]{2,1,0:T(8,128)} %pad.93) | copy-start | bytes 5505028
  152.1 14.5 %copy-start.8 = (f32[8,8192]{1,0:T(8,128)S(1)}, f32[8,8192]{1,0:T(8,128)}, u32[]{:S(2)}) copy-start(f32[8,8192]{1,0:T(8,128)} %get-tuple-element.24) | copy-start | bytes 786436
  152.1 14.5 %copy-start.11 = (pred[8,8192]{1,0:T(8,128)(4,1)S(1)}, pred[8,8192]{1,0:T(8,128)(4,1)}, u32[]{:S(2)}) copy-start(pred[8,8192]{1,0:T(8,128)(4,1)} %broadcast_compare_fusion) | copy-start | bytes 196612
where the time goes:
time: 172 us; the launch traced here: 171 us
  blocking collectives  105 us (61%)
  local copies, waits for them, and re-layouts  35.3 us (21%)
  other arithmetic  30.2 us (18%)
    all_gather x8, blocking collectives, entering(): pieces = jax.tree.map(lambda part: lax.all_gather(part, axis), subtotal)  105 us
    pad x8, local copies, waits for them, and re-layouts, scan_block(): lax.associative_scan(pass_forward, (jnp.where(live, day_col, -1), values)...  9.38 us
    slice x9, local copies, waits for them, and re-layouts, scan_block(): lax.associative_scan(pass_backward, (jnp.where(live, day_col, far_day), v...  8.14 us
    pad x8, local copies, waits for them, and re-layouts, scan_block(): lax.associative_scan(pass_backward, (jnp.where(live, day_col, far_day), v...  5.61 us
    add x7, other arithmetic, scan_block(): lax.associative_scan(pass_backward, (jnp.where(live, day_col, far_day), v...  5.25 us
    slice x7, local copies, waits for them, and re-layouts, scan_block(): lax.associative_scan(pass_forward, (jnp.where(live, day_col, -1), values)...  4.45 us
    unnamed x65, local copies, waits for them, and re-layouts  4.42 us

commit v1 on v0

v1 whole, which is shorter than its diff:
```python
import functools

import jax
import jax.numpy as jnp
from jax import lax
from jax.experimental import pallas as pl
from jax.experimental.pallas import tpu as pltpu
from jax.sharding import Mesh
from jax.sharding import PartitionSpec as P

MESH = pl.DeviceIdType.MESH
DATE = ("date_0", "date_1")
LANES = 128
ROWS = 8
TILES = 4
STAGES = 4
LAG = 3
NONE = -1073741824.0


def spread(row):
    return jnp.broadcast_to(row, (ROWS, LANES))


def scan_fill(
    bands,
    chunks,
    days_hbm,
    x_hbm,
    v_hbm,
    out_ref,
    days,
    xv,
    vv,
    own,
    come,
    enter,
    day_sem,
    x_sem,
    v_sem,
    send_sem,
    recv_sem,
):
    width = TILES * LANES
    yi = lax.axis_index(DATE[0])
    xi = lax.axis_index(DATE[1])
    partner = (
        {DATE[1]: xi + 1 - 2 * lax.rem(xi, 2)},
        {DATE[1]: 3 - xi},
        {DATE[0]: yi + 1 - 2 * lax.rem(yi, 2)},
        {DATE[0]: 3 - yi},
    )
    upper = (lax.rem(xi, 2), xi // 2, lax.rem(yi, 2), yi // 2)

    def load_x(c):
        cols = pl.ds(pl.multiple_of(c * width, width), width)
        return pltpu.make_async_copy(x_hbm.at[:, :, cols], xv.at[:, :, cols], x_sem.at[c])

    def load_v(c):
        cols = pl.ds(pl.multiple_of(c * width, width), width)
        return pltpu.make_async_copy(v_hbm.at[:, cols], vv.at[:, cols], v_sem.at[c])

    def exchange(stage, c):
        return pltpu.make_async_remote_copy(
            src_ref=own.at[stage, c],
            dst_ref=come.at[stage, c],
            send_sem=send_sem.at[stage, c],
            recv_sem=recv_sem.at[stage, c],
            device_id=partner[stage],
            device_id_type=MESH,
        )

    day_copy = pltpu.make_async_copy(days_hbm, days, day_sem)
    day_copy.start()

    @pl.loop(0, chunks)
    def _(c):
        load_v(c).start()
        load_x(c).start()

    barrier = pltpu.get_barrier_semaphore()
    for who in partner:
        pl.semaphore_signal(barrier, inc=1, device_id=who, device_id_type=MESH)

    day_copy.wait()
    sub = lax.broadcasted_iota(jnp.int32, (ROWS, LANES), 0)
    day_col = jnp.zeros((ROWS, LANES), jnp.float32)
    for t in range(ROWS):
        day_col = jnp.where(sub == t, days[t].astype(jnp.float32), day_col)
    lower_rows = sub < TILES
    pl.semaphore_wait(barrier, len(partner))

    def summarize(c):
        load_v(c).wait()
        load_x(c).wait()
        for j in range(TILES):
            cols = pl.ds(pl.multiple_of(c * width + j * LANES, LANES), LANES)
            live = vv[:, cols] > 0
            last = jnp.max(jnp.where(live, day_col, NONE), axis=0, keepdims=True)
            first = jnp.max(jnp.where(live, -day_col, NONE), axis=0, keepdims=True)
            own[0, c, bands, pl.ds(j, 1), :] = last
            own[0, c, bands, pl.ds(TILES + j, 1), :] = first
            at_last = day_col == spread(last)
            at_first = -day_col == spread(first)
            for b in range(bands):
                x = xv[b, :, cols]
                own[0, c, b, pl.ds(j, 1), :] = jnp.sum(
                    jnp.where(at_last, x, 0.0), axis=0, keepdims=True
                )
                own[0, c, b, pl.ds(TILES + j, 1), :] = jnp.sum(
                    jnp.where(at_first, x, 0.0), axis=0, keepdims=True
                )
        exchange(0, c).start()

    def merge(stage, c):
        exchange(stage, c).wait_recv()
        near = lower_rows == (jnp.full((ROWS, LANES), upper[stage], jnp.int32) > 0)
        key = own[stage, c, bands]
        other = come[stage, c, bands]
        if stage + 1 < STAGES:
            take = other > key
            for b in range(bands + 1):
                own[stage + 1, c, b] = jnp.where(take, come[stage, c, b], own[stage, c, b])
            exchange(stage + 1, c).start()
        if stage == 0:
            take = near & (other > NONE)
            for b in range(bands):
                enter[c, b] = jnp.where(take, come[stage, c, b], 0.0)
            enter[c, bands] = jnp.where(take, other, NONE)
        else:
            take = near & (other > enter[c, bands])
            for b in range(bands + 1):
                enter[c, b] = jnp.where(take, come[stage, c, b], enter[c, b])

    def complete(c):
        e_key = enter[c, bands]
        o_key = own[0, c, bands]
        e_has = e_key > NONE
        o_has = o_key > NONE
        flip = functools.partial(pltpu.roll, shift=TILES, axis=0)
        for b in range(bands):
            e = enter[c, b]
            enter[c, b] = jnp.where(e_has, e, flip(jnp.where(o_has, own[0, c, b], e)))
        e_day = jnp.where(lower_rows, e_key, -e_key)
        o_day = jnp.where(lower_rows, o_key, -o_key)
        enter[c, bands] = jnp.where(e_has, e_day, flip(jnp.where(o_has, o_day, e_day)))
        for j in range(TILES):
            cols = pl.ds(pl.multiple_of(c * width + j * LANES, LANES), LANES)
            live = vv[:, cols] > 0
            before = jnp.where(live, sub, -1)
            after = jnp.where(live, sub, ROWS)
            for k in (1, 2, 4):
                before = jnp.maximum(
                    before, jnp.where(sub >= k, pltpu.roll(before, k, axis=0), -1)
                )
                after = jnp.minimum(
                    after, jnp.where(sub < ROWS - k, pltpu.roll(after, ROWS - k, axis=0), ROWS)
                )
            has_f = before >= 0
            has_b = after < ROWS
            at_f = jnp.maximum(before, 0)
            at_b = jnp.minimum(after, ROWS - 1)

            def sides(x, b):
                f = jnp.take_along_axis(x, at_f, axis=0)
                n = jnp.take_along_axis(x, at_b, axis=0)
                f = jnp.where(has_f, f, spread(enter[c, b, pl.ds(j, 1), :]))
                n = jnp.where(has_b, n, spread(enter[c, b, pl.ds(TILES + j, 1), :]))
                return f, n

            prev, following = sides(day_col, bands)
            span = following - prev
            weight = (day_col - prev) / jnp.where(span == 0.0, 1.0, span)
            for b in range(bands):
                f, n = sides(xv[b, :, cols], b)
                out_ref[b, :, cols] = f + weight * (n - f)

    @pl.loop(0, chunks)
    def _(c):
        summarize(c)

    @pl.loop(0, chunks + LAG * (STAGES - 1))
    def _(t):
        for stage in range(STAGES):
            c = t - LAG * stage

            @pl.when((c >= 0) & (c < chunks))
            def _():
                merge(stage, c)
                if stage == STAGES - 1:
                    complete(c)

    @pl.loop(0, chunks)
    def _(c):
        for stage in range(STAGES):
            exchange(stage, c).wait_send()


def body(reflectance, validity, day_number):
    dates, bands, pixels = reflectance.shape
    chunks = pixels // (TILES * LANES)
    hbm = pl.BlockSpec(memory_space=pltpu.HBM)
    filled = pl.pallas_call(
        functools.partial(scan_fill, bands, chunks),
        out_shape=pltpu.VMEM((bands, dates, pixels), jnp.float32),
        in_specs=[hbm, hbm, hbm],
        out_specs=pl.BlockSpec(memory_space=pltpu.VMEM),
        scratch_shapes=[
            pltpu.SMEM((dates,), jnp.int32),
            pltpu.VMEM((bands, dates, pixels), jnp.float32),
            pltpu.VMEM((dates, pixels), jnp.int32),
            pltpu.VMEM((STAGES, chunks, bands + 1, ROWS, LANES), jnp.float32),
            pltpu.VMEM((STAGES, chunks, bands + 1, ROWS, LANES), jnp.float32),
            pltpu.VMEM((chunks, bands + 1, ROWS, LANES), jnp.float32),
            pltpu.SemaphoreType.DMA,
            pltpu.SemaphoreType.DMA((chunks,)),
            pltpu.SemaphoreType.DMA((chunks,)),
            pltpu.SemaphoreType.DMA((STAGES, chunks)),
            pltpu.SemaphoreType.DMA((STAGES, chunks)),
        ],
        compiler_params=pltpu.CompilerParams(
            collective_id=0, has_side_effects=True, vmem_limit_bytes=(62 << 20) - 65536
        ),
        name="scan_fill",
    )(day_number, jnp.transpose(reflectance, (1, 0, 2)), validity)
    return jnp.transpose(filled, (1, 0, 2))


def solution(mesh):
    torus = Mesh(
        mesh.devices.reshape(4, 4, mesh.shape["pix"], mesh.shape["tile"]),
        ("date_0", "date_1", "pix", "tile"),
    )
    placed = (P(DATE, None, ("tile", "pix")), P(DATE, ("tile", "pix")), P(DATE))
    return jax.shard_map(
        body, mesh=torus, in_specs=placed, out_specs=P(DATE, None, ("tile", "pix")), check_vma=False
    )
```

time: 172 us -> 35.2 us (0.20)
  blocking collectives: 105 us -> 0 us
  local copies, waits for them, and re-layouts: 35.3 us -> 1.23 us
  Pallas kernels: 0 us -> 33.9 us
  other arithmetic: 30.2 us -> 0 us
    all_gather x8 -> x0, blocking collectives: 105 us -> none  [entering(): pieces = jax.tree.map(lambda part: lax.all_gather(part, axis), subtotal)]
    pallas_call x0 -> x1, Pallas kernels: none -> 33.9 us  [body(): pl.pallas_call(functools.partial(scan_fill, bands, chunks), out_shape=plt...]
    pad x16 -> x0, local copies, waits for them, and re-layouts: 15 us -> none  [the longest x8 9.38 us: scan_block(): lax.associative_scan(pass_forward, (jnp.where(live, day_col, -1), values)...]
    slice x16 -> x0, local copies, waits for them, and re-layouts: 12.6 us -> none  [the longest x9 8.14 us: scan_block(): lax.associative_scan(pass_backward, (jnp.where(live, day_col, far_day), v...]
    select_n x21 -> x0, other arithmetic: 8.48 us -> none  [the longest x4 2.82 us: pass_forward(): jnp.where(keep[:, None, :], later[1], earlier[1])]
    add x12 -> x0, other arithmetic: 8.33 us -> none  [the longest x7 5.25 us: scan_block(): lax.associative_scan(pass_backward, (jnp.where(live, day_col, far_day), v...]
    lt x9 -> x0, other arithmetic: 4.35 us -> none  [the longest x3 2.74 us: take_backward(): keep = later[0] < far_day]
    concatenate x8 -> x0, other arithmetic: 4.12 us -> none  [the longest x4 2.09 us: scan_block(): lax.associative_scan(pass_forward, (jnp.where(live, day_col, -1), values)...]
where the time goes in v1:
time: 35.2 us; the launch traced here: 35.1 us
  Pallas kernels  33.9 us (96%)
  local copies, waits for them, and re-layouts  1.23 us (3%)
    pallas_call x1, Pallas kernels, body(): pl.pallas_call(functools.partial(scan_fill, bands, chunks), out_shape=plt...  33.9 us
    unnamed x1, local copies, waits for them, and re-layouts  1.23 us

profile of v1, /device:TPU:0, one launch (start us, length us, event | category | flops | bytes accessed | tf_op | source)
XLA Modules:
  0.0 35.1 jit_solution(5147352708854566321)
XLA Ops:
  0.0 33.9 %scan_fill.1 = f32[7,8,8192]{2,1,0:T(8,128)S(1)} custom-call(s32[8]{0:T(128)} %days_hbm.1, f32[7,8,8192]{2,1,0:T(8,128)} %bitcast.3, s32[8,8192]{1,0:T(8,128)} %v_hbm.1), custom_call_target="tpu_custom_call" | custom-call | tf_op jit(solution)/shard_map/scan_fill/pallas_call | solution.py:203
  33.9 1.2 %copy.5 = f32[8,7,8192]{2,0,1:T(8,128)} copy(f32[8,7,8192]{2,0,1:T(8,128)S(1)} %bitcast.2) | data formatting | bytes 3670016

commit v2 on v1

v2 whole, which is shorter than its diff:
```python
import functools

import jax
import jax.numpy as jnp
from jax import lax
from jax.experimental import pallas as pl
from jax.experimental.pallas import tpu as pltpu
from jax.sharding import Mesh
from jax.sharding import PartitionSpec as P

MESH = pl.DeviceIdType.MESH
DATE = ("date_0", "date_1")
LANES = 128
ROWS = 8
TILES = 4
SIDE = 4
NONE = -1073741824.0
SHARES = (1, 1, 2, 2, 2, 2, 2, 2, 1, 1)
LOADS = (1, 1, 2, 4, 8)
STEP, HOP, FAR = 0.7, 2.4, 3.2


def spans(shares, groups):
    scale = groups // sum(shares) if groups >= sum(shares) else 0
    if scale == 0:
        return [(g, 1) for g in range(groups)]
    starts, at = [], 0
    for share in shares:
        starts.append((at, share * scale))
        at += share * scale
    return starts


def arrival_order(messages):
    events, ready = [], [0.0] * len(messages)
    for stage, delay in enumerate((HOP, HOP, FAR)):
        link = 0.0
        for m, (_, count) in enumerate(messages):
            link = max(link, ready[m]) + STEP * count
            ready[m] = link + delay
            events.append((ready[m], stage, m))
    return [(stage, m) for _, stage, m in sorted(events)]


def scan_fill(
    bands,
    groups,
    days_hbm,
    x_hbm,
    v_hbm,
    out_ref,
    days,
    xv,
    vv,
    own,
    come,
    come_y,
    enter,
    day_sem,
    x_sem,
    v_sem,
    send_sem,
    recv_sem,
):
    width = TILES * LANES
    packs = (bands + 1) // 2
    messages, loads = spans(SHARES, groups), spans(LOADS, groups)
    yi = lax.axis_index(DATE[0])
    xi = lax.axis_index(DATE[1])
    pair = ({DATE[1]: xi + 1 - 2 * lax.rem(xi, 2)}, {DATE[1]: 3 - xi})
    taken = (1 - lax.rem(xi, 2), 1 - xi // 2)
    rows = [{DATE[0]: lax.rem(yi + d, SIDE)} for d in range(1, SIDE)]
    row_gives = [(yi + d) // SIDE for d in range(1, SIDE)]
    row_takes = [1 - (yi + SIDE - d) // SIDE for d in range(1, SIDE)]

    def load_x(i):
        cols = pl.ds(loads[i][0] * width, loads[i][1] * width)
        return pltpu.make_async_copy(x_hbm.at[:, :, cols], xv.at[:, :, cols], x_sem.at[i])

    def load_v(i):
        cols = pl.ds(loads[i][0] * width, loads[i][1] * width)
        return pltpu.make_async_copy(v_hbm.at[:, cols], vv.at[:, cols], v_sem.at[i])

    def swap(stage, m):
        part = pl.ds(*messages[m])
        return pltpu.make_async_remote_copy(
            src_ref=own.at[stage, part],
            dst_ref=come.at[stage, part],
            send_sem=send_sem.at[stage],
            recv_sem=recv_sem.at[stage, m],
            device_id=pair[stage],
            device_id_type=MESH,
        )

    def to_row(d, m):
        part = pl.ds(*messages[m])
        return pltpu.make_async_remote_copy(
            src_ref=own.at[2, part, row_gives[d]],
            dst_ref=come_y.at[part, d],
            send_sem=send_sem.at[2],
            recv_sem=recv_sem.at[2, m],
            device_id=rows[d],
            device_id_type=MESH,
        )

    def from_rows(part, m):
        return pltpu.make_async_remote_copy(
            src_ref=come_y.at[part],
            dst_ref=come_y.at[part],
            send_sem=send_sem.at[2],
            recv_sem=recv_sem.at[2, m],
            device_id=rows[0],
            device_id_type=MESH,
        )

    barrier = pltpu.get_barrier_semaphore()
    for who in (*pair, *rows):
        pl.semaphore_signal(barrier, inc=1, device_id=who, device_id_type=MESH)
    day_copy = pltpu.make_async_copy(days_hbm, days, day_sem)
    day_copy.start()
    for i in range(len(loads)):
        load_v(i).start()
        load_x(i).start()

    day_copy.wait()
    sub = lax.broadcasted_iota(jnp.int32, (ROWS, LANES), 0)
    day_col = jnp.zeros((ROWS, LANES), jnp.float32)
    for t in range(ROWS):
        day_col = jnp.where(sub == t, days[t].astype(jnp.float32), day_col)
    key_rows = sub >= TILES

    def lanes_of(g, j):
        return pl.ds(pl.multiple_of(g * width + j * LANES, LANES), LANES)

    def key_of(pack):
        return jnp.where(key_rows, pack, pltpu.roll(pack, TILES, axis=0))

    def spread(row):
        return jnp.broadcast_to(row, (ROWS, LANES))

    def row_of(band, j):
        return band // 2, pl.ds((band % 2) * TILES + j, 1)

    def over(m, work):
        start, count = messages[m]
        if count == 1:
            work(start)
        else:
            pl.loop(start, start + count)(work)

    def summarize(g):
        for j in range(TILES):
            cols = lanes_of(g, j)
            live = vv[:, cols] > 0
            last = jnp.max(jnp.where(live, day_col, NONE), axis=0, keepdims=True)
            first = jnp.max(jnp.where(live, -day_col, NONE), axis=0, keepdims=True)
            at_last = day_col == spread(last)
            at_first = -day_col == spread(first)
            for b in range(bands):
                x = xv[b, :, cols]
                p, r = row_of(b, j)
                own[0, g, 0, p, r, :] = jnp.sum(jnp.where(at_last, x, 0.0), axis=0, keepdims=True)
                own[0, g, 1, p, r, :] = jnp.sum(jnp.where(at_first, x, 0.0), axis=0, keepdims=True)
            p, r = row_of(bands, j)
            own[0, g, 0, p, r, :] = last
            own[0, g, 1, p, r, :] = first

    def merge_pair(stage, g):
        for side in range(2):
            take = key_of(come[stage, g, side, packs - 1]) > key_of(own[stage, g, side, packs - 1])
            for p in range(packs):
                own[stage + 1, g, side, p] = jnp.where(
                    take, come[stage, g, side, p], own[stage, g, side, p]
                )

    def note_pair(stage, g):
        side = taken[stage]
        if stage == 0:
            for p in range(packs):
                enter[g, side, p] = come[0, g, side, p]
                enter[g, 1 - side, p] = jnp.where(key_rows, NONE if p == packs - 1 else 0.0, 0.0)
        else:
            take = key_of(come[stage, g, side, packs - 1]) > key_of(enter[g, side, packs - 1])
            for p in range(packs):
                enter[g, side, p] = jnp.where(take, come[stage, g, side, p], enter[g, side, p])

    def complete(g):
        for d in range(SIDE - 1):
            side = row_takes[d]
            take = key_of(come_y[g, d, packs - 1]) > key_of(enter[g, side, packs - 1])
            for p in range(packs):
                enter[g, side, p] = jnp.where(take, come_y[g, d, p], enter[g, side, p])
        has = [key_of(enter[g, s, packs - 1]) > NONE for s in range(2)]
        mine = [key_of(own[0, g, s, packs - 1]) > NONE for s in range(2)]
        for p in range(packs):
            ends = [enter[g, s, p] for s in range(2)]
            other = [jnp.where(mine[s], own[0, g, s, p], ends[s]) for s in range(2)]
            if p == packs - 1:
                other = [jnp.where(key_rows, -o, o) for o in other]
            for s in range(2):
                enter[g, s, p] = jnp.where(has[s], ends[s], other[1 - s])
        for j in range(TILES):
            cols = lanes_of(g, j)
            live = vv[:, cols] > 0
            before = jnp.where(live, sub, -1)
            after = jnp.where(live, sub, ROWS)
            for k in (1, 2, 4):
                before = jnp.maximum(
                    before, jnp.where(sub >= k, pltpu.roll(before, k, axis=0), -1)
                )
                after = jnp.minimum(
                    after, jnp.where(sub < ROWS - k, pltpu.roll(after, ROWS - k, axis=0), ROWS)
                )
            has_f = before >= 0
            has_b = after < ROWS
            at_f = jnp.maximum(before, 0)
            at_b = jnp.minimum(after, ROWS - 1)

            def sides(x, b, sign):
                p, r = row_of(b, j)
                f = jnp.take_along_axis(x, at_f, axis=0)
                n = jnp.take_along_axis(x, at_b, axis=0)
                f = jnp.where(has_f, f, spread(enter[g, 0, p, r, :]))
                n = jnp.where(has_b, n, spread(sign * enter[g, 1, p, r, :]))
                return f, n

            prev, following = sides(day_col, bands, -1.0)
            span = following - prev
            weight = (day_col - prev) / jnp.where(span == 0.0, 1.0, span)
            for b in range(bands):
                f, n = sides(xv[b, :, cols], b, 1.0)
                out_ref[b, :, cols] = f + weight * (n - f)

    loaded = 0
    for m, (start, count) in enumerate(messages):
        while loaded < len(loads) and loads[loaded][0] < start + count:
            load_v(loaded).wait()
            load_x(loaded).wait()
            loaded += 1
        over(m, summarize)
        if m == 0:
            pl.semaphore_wait(barrier, len(pair) + len(rows))
        swap(0, m).start()

    for stage, m in arrival_order(messages):
        if stage < 2:
            swap(stage, m).wait_recv()
            over(m, functools.partial(merge_pair, stage))
            if stage == 0:
                swap(1, m).start()
            else:
                for d in range(SIDE - 1):
                    to_row(d, m).start()
            over(m, functools.partial(note_pair, stage))
        else:
            from_rows(pl.ds(*messages[m]), m).wait_recv()
            over(m, complete)

    for stage in range(2):
        pltpu.make_async_remote_copy(
            src_ref=own.at[stage],
            dst_ref=come.at[stage],
            send_sem=send_sem.at[stage],
            recv_sem=recv_sem.at[stage, 0],
            device_id=pair[stage],
            device_id_type=MESH,
        ).wait_send()
    from_rows(pl.ds(0, groups), 0).wait_send()


def body(reflectance, validity, day_number):
    dates, bands, pixels = reflectance.shape
    groups = pixels // (TILES * LANES)
    packs = (bands + 1) // 2
    messages, loads = len(spans(SHARES, groups)), len(spans(LOADS, groups))
    hbm = pl.BlockSpec(memory_space=pltpu.HBM)
    filled = pl.pallas_call(
        functools.partial(scan_fill, bands, groups),
        out_shape=pltpu.VMEM((bands, dates, pixels), jnp.float32),
        in_specs=[hbm, hbm, hbm],
        out_specs=pl.BlockSpec(memory_space=pltpu.VMEM),
        scratch_shapes=[
            pltpu.SMEM((dates,), jnp.int32),
            pltpu.VMEM((bands, dates, pixels), jnp.float32),
            pltpu.VMEM((dates, pixels), jnp.int32),
            pltpu.VMEM((3, groups, 2, packs, ROWS, LANES), jnp.float32),
            pltpu.VMEM((2, groups, 2, packs, ROWS, LANES), jnp.float32),
            pltpu.VMEM((groups, SIDE - 1, packs, ROWS, LANES), jnp.float32),
            pltpu.VMEM((groups, 2, packs, ROWS, LANES), jnp.float32),
            pltpu.SemaphoreType.DMA,
            pltpu.SemaphoreType.DMA((loads,)),
            pltpu.SemaphoreType.DMA((loads,)),
            pltpu.SemaphoreType.DMA((3,)),
            pltpu.SemaphoreType.DMA((3, messages)),
        ],
        compiler_params=pltpu.CompilerParams(
            collective_id=0, has_side_effects=True, vmem_limit_bytes=(62 << 20) - 65536
        ),
        name="scan_fill",
    )(day_number, jnp.transpose(reflectance, (1, 0, 2)), validity)
    return jnp.transpose(filled, (1, 0, 2))


def solution(mesh):
    torus = Mesh(
        mesh.devices.reshape(4, 4, mesh.shape["pix"], mesh.shape["tile"]),
        ("date_0", "date_1", "pix", "tile"),
    )
    placed = (P(DATE, None, ("tile", "pix")), P(DATE, ("tile", "pix")), P(DATE))
    return jax.shard_map(
        body, mesh=torus, in_specs=placed, out_specs=P(DATE, None, ("tile", "pix")), check_vma=False
    )
```

time: 35.2 us -> 27.4 us (0.78)
  Pallas kernels: 33.9 us -> 26 us
    pallas_call x1, Pallas kernels: 33.9 us -> 26 us  [body(): pl.pallas_call(functools.partial(scan_fill, bands, groups), out_shape=plt...]
where the time goes in v2:
time: 27.4 us; the launch traced here: 27.2 us
  Pallas kernels  26 us (95%)
  local copies, waits for them, and re-layouts  1.23 us (4%)
    pallas_call x1, Pallas kernels, body(): pl.pallas_call(functools.partial(scan_fill, bands, groups), out_shape=plt...  26 us
    unnamed x1, local copies, waits for them, and re-layouts  1.23 us

profile of v2, /device:TPU:0, one launch (start us, length us, event | category | flops | bytes accessed | tf_op | source)
XLA Modules:
  0.0 27.2 jit_solution(5942498801052806103)
XLA Ops:
  0.0 26.0 %scan_fill.1 = f32[7,8,8192]{2,1,0:T(8,128)S(1)} custom-call(s32[8]{0:T(128)} %days_hbm.1, f32[7,8,8192]{2,1,0:T(8,128)} %bitcast.3, s32[8,8192]{1,0:T(8,128)} %v_hbm.1), custom_call_target="tpu_custom_call" | custom-call | tf_op jit(solution)/shard_map/scan_fill/pallas_call | solution.py:277
  26.0 1.2 %copy.5 = f32[8,7,8192]{2,0,1:T(8,128)} copy(f32[8,7,8192]{2,0,1:T(8,128)S(1)} %bitcast.2) | data formatting | bytes 3670016

commit v3 on v2

--- a/solution.py
+++ b/solution.py
@@ -16,8 +16,8 @@
 SIDE = 4
 NONE = -1073741824.0
 SHARES = (1, 1, 2, 2, 2, 2, 2, 2, 1, 1)
-LOADS = (1, 1, 2, 4, 8)
-STEP, HOP, FAR = 0.7, 2.4, 3.2
+LOADS = (2, 6, 8)
+STEP, HOP, FAR = 0.7, 3.0, 3.8
 
 
 def spans(shares, groups):

time: 27.4 us -> 26.8 us (0.978)
  Pallas kernels: 26 us -> 25.4 us
    pallas_call x1, Pallas kernels: 26 us -> 25.4 us  [body(): pl.pallas_call(functools.partial(scan_fill, bands, groups), out_shape=plt...]
where the time goes in v3:
time: 26.8 us; the launch traced here: 26.6 us
  Pallas kernels  25.4 us (95%)
  local copies, waits for them, and re-layouts  1.23 us (5%)
    pallas_call x1, Pallas kernels, body(): pl.pallas_call(functools.partial(scan_fill, bands, groups), out_shape=plt...  25.4 us
    unnamed x1, local copies, waits for them, and re-layouts  1.23 us

profile of v3, /device:TPU:0, one launch (start us, length us, event | category | flops | bytes accessed | tf_op | source)
XLA Modules:
  0.0 26.6 jit_solution(15666132209426148489)
XLA Ops:
  0.0 25.4 %scan_fill.1 = f32[7,8,8192]{2,1,0:T(8,128)S(1)} custom-call(s32[8]{0:T(128)} %days_hbm.1, f32[7,8,8192]{2,1,0:T(8,128)} %bitcast.3, s32[8,8192]{1,0:T(8,128)} %v_hbm.1), custom_call_target="tpu_custom_call" | custom-call | tf_op jit(solution)/shard_map/scan_fill/pallas_call | solution.py:277
  25.4 1.2 %copy.5 = f32[8,7,8192]{2,0,1:T(8,128)} copy(f32[8,7,8192]{2,0,1:T(8,128)S(1)} %bitcast.2) | data formatting | bytes 3670016

commit v4 on v3

--- a/solution.py
+++ b/solution.py
@@ -15,31 +15,61 @@
 TILES = 4
 SIDE = 4
 NONE = -1073741824.0
-SHARES = (1, 1, 2, 2, 2, 2, 2, 2, 1, 1)
+STRAIGHT, TURNED = 1, 2
+SHARES = (-1, 1, 2, 2, 2, 2, 1, 1, -1)
 LOADS = (2, 6, 8)
-STEP, HOP, FAR = 0.7, 3.0, 3.8
-
-
-def spans(shares, groups):
-    scale = groups // sum(shares) if groups >= sum(shares) else 0
-    if scale == 0:
+UNIT, HOP, FAR = 0.35, 3.0, 4.0
+EARLY, MIDDLE = 5, 10
+TURN = 16
+
+
+def pieces(shares, groups):
+    if sum(abs(s) for s in shares) != groups:
         return [(g, 1) for g in range(groups)]
     starts, at = [], 0
     for share in shares:
-        starts.append((at, share * scale))
-        at += share * scale
+        starts.append((at, abs(share)))
+        at += abs(share)
     return starts
 
 
-def arrival_order(messages):
-    events, ready = [], [0.0] * len(messages)
-    for stage, delay in enumerate((HOP, HOP, FAR)):
-        link = 0.0
-        for m, (_, count) in enumerate(messages):
-            link = max(link, ready[m]) + STEP * count
-            ready[m] = link + delay
-            events.append((ready[m], stage, m))
-    return [(stage, m) for _, stage, m in sorted(events)]
+def plan(groups):
+    across, turned = (STRAIGHT, TURNED) if groups > STRAIGHT + TURNED else (1, 1)
+    hyper = groups - across - turned
+    parts = pieces(SHARES, hyper)
+    split = [s < 0 for s in SHARES] if len(parts) == len(SHARES) else [False] * len(parts)
+    messages, owner = [], []
+    for r, (start, count) in enumerate(parts):
+        for side in (0, 1) if split[r] else (None,):
+            messages.append((start, count, side or 0, 2 if side is None else 1))
+            owner.append(r)
+    rows = [*parts, (hyper, across), (hyper + across, turned)]
+    load = 2 * across * UNIT
+    events, first, second = [], 0.0, 2 * load
+    ready, straight = [], 0.0
+    for i, m in enumerate(messages):
+        if i == min(EARLY, len(messages) - 1):
+            first += load
+        if i == min(MIDDLE, len(messages) - 1):
+            first += load
+            straight = first + HOP
+        first += m[1] * m[3] * UNIT
+        ready.append(first + HOP)
+        events.append((ready[i], 0, i))
+    events.append((straight, 2, 0))
+    done = [0.0] * (len(rows) - 1)
+    done[-1] = straight
+    for i, m in enumerate(messages):
+        second = max(second, ready[i]) + m[1] * m[3] * UNIT
+        events.append((second + HOP, 1, i))
+        done[owner[i]] = second + HOP
+    link = 0.0
+    for r in sorted(range(len(done)), key=lambda r: done[r]):
+        link = max(link, done[r]) + 2 * UNIT * rows[r][1]
+        events.append((link + FAR, 3, r))
+    events.append((TURN, 4, 0))
+    events.append((max(TURN, first, second) + 4 * turned * UNIT + FAR, 5, 0))
+    return messages, owner, rows, [(kind, i) for _, kind, i in sorted(events)]
 
 
 def scan_fill(
@@ -54,6 +84,7 @@
     vv,
     own,
     come,
+    come_x,
     come_y,
     enter,
     day_sem,
@@ -64,7 +95,10 @@
 ):
     width = TILES * LANES
     packs = (bands + 1) // 2
-    messages, loads = spans(SHARES, groups), spans(LOADS, groups)
+    loads = pieces(LOADS, groups)
+    messages, owner, row_parts, order = plan(groups)
+    straight, turned = row_parts[-2:]
+    places = (pl.ds(0, straight[1]), pl.ds(straight[1], turned[1]))
     yi = lax.axis_index(DATE[0])
     xi = lax.axis_index(DATE[1])
     pair = ({DATE[1]: xi + 1 - 2 * lax.rem(xi, 2)}, {DATE[1]: 3 - xi})
@@ -72,6 +106,8 @@
     rows = [{DATE[0]: lax.rem(yi + d, SIDE)} for d in range(1, SIDE)]
     row_gives = [(yi + d) // SIDE for d in range(1, SIDE)]
     row_takes = [1 - (yi + SIDE - d) // SIDE for d in range(1, SIDE)]
+    crossing = (pair[1], {DATE[1]: lax.rem(xi + 2, SIDE)}, pair[0])
+    cross_takes = (1 - xi // 2, 1 - xi // 2, 1 - lax.rem(xi, 2))
 
     def load_x(i):
         cols = pl.ds(loads[i][0] * width, loads[i][1] * width)
@@ -82,39 +118,63 @@
         return pltpu.make_async_copy(v_hbm.at[:, cols], vv.at[:, cols], v_sem.at[i])
 
     def swap(stage, m):
-        part = pl.ds(*messages[m])
+        start, count, side, sides = messages[m]
+        part, which = pl.ds(start, count), pl.ds(side, sides)
         return pltpu.make_async_remote_copy(
-            src_ref=own.at[stage, part],
-            dst_ref=come.at[stage, part],
+            src_ref=own.at[stage, part, which],
+            dst_ref=come.at[stage, part, which],
             send_sem=send_sem.at[stage],
-            recv_sem=recv_sem.at[stage, m],
+            recv_sem=recv_sem.at[stage * len(messages) + m],
             device_id=pair[stage],
             device_id_type=MESH,
         )
 
-    def to_row(d, m):
-        part = pl.ds(*messages[m])
+    def cross(turn, i):
         return pltpu.make_async_remote_copy(
-            src_ref=own.at[2, part, row_gives[d]],
+            src_ref=own.at[1 + cross_takes[i], pl.ds(*turned)] if turn else own.at[0, pl.ds(*straight)],
+            dst_ref=come_x.at[i, places[turn]],
+            send_sem=send_sem.at[2],
+            recv_sem=recv_sem.at[2 * len(messages) + turn],
+            device_id=crossing[i],
+            device_id_type=MESH,
+        )
+
+    def crossed(part, turn):
+        return pltpu.make_async_remote_copy(
+            src_ref=part,
+            dst_ref=part,
+            send_sem=send_sem.at[2],
+            recv_sem=recv_sem.at[2 * len(messages) + turn],
+            device_id=crossing[0],
+            device_id_type=MESH,
+        )
+
+    def row_sem(r):
+        return recv_sem.at[2 * len(messages) + 2 + r]
+
+    def to_row(d, r):
+        part = pl.ds(*row_parts[r])
+        return pltpu.make_async_remote_copy(
+            src_ref=own.at[0 if r == len(row_parts) - 1 else 2, part, row_gives[d]],
             dst_ref=come_y.at[part, d],
-            send_sem=send_sem.at[2],
-            recv_sem=recv_sem.at[2, m],
+            send_sem=send_sem.at[3],
+            recv_sem=row_sem(r),
             device_id=rows[d],
             device_id_type=MESH,
         )
 
-    def from_rows(part, m):
+    def from_rows(part, r):
         return pltpu.make_async_remote_copy(
             src_ref=come_y.at[part],
             dst_ref=come_y.at[part],
-            send_sem=send_sem.at[2],
-            recv_sem=recv_sem.at[2, m],
+            send_sem=send_sem.at[3],
+            recv_sem=row_sem(r),
             device_id=rows[0],
             device_id_type=MESH,
         )
 
     barrier = pltpu.get_barrier_semaphore()
-    for who in (*pair, *rows):
+    for who in (*crossing, *rows):
         pl.semaphore_signal(barrier, inc=1, device_id=who, device_id_type=MESH)
     day_copy = pltpu.make_async_copy(days_hbm, days, day_sem)
     day_copy.start()
@@ -141,8 +201,7 @@
     def row_of(band, j):
         return band // 2, pl.ds((band % 2) * TILES + j, 1)
 
-    def over(m, work):
-        start, count = messages[m]
+    def over(start, count, work):
         if count == 1:
             work(start)
         else:
@@ -165,31 +224,75 @@
             own[0, g, 0, p, r, :] = last
             own[0, g, 1, p, r, :] = first
 
-    def merge_pair(stage, g):
-        for side in range(2):
+    def merge_pair(stage, sides, g):
+        for side in sides:
             take = key_of(come[stage, g, side, packs - 1]) > key_of(own[stage, g, side, packs - 1])
             for p in range(packs):
                 own[stage + 1, g, side, p] = jnp.where(
                     take, come[stage, g, side, p], own[stage, g, side, p]
                 )
 
-    def note_pair(stage, g):
-        side = taken[stage]
-        if stage == 0:
+    def enter_less(g, side, packs_of):
+        take = key_of(packs_of(packs - 1)) > key_of(enter[g, side, packs - 1])
+        for p in range(packs):
+            enter[g, side, p] = jnp.where(take, packs_of(p), enter[g, side, p])
+
+    def clear(g, side):
+        for p in range(packs):
+            enter[g, side, p] = jnp.where(key_rows, NONE if p == packs - 1 else 0.0, 0.0)
+
+    def note_pair(g):
+        side = taken[0]
+        clear(g, 1 - side)
+        for p in range(packs):
+            enter[g, side, p] = come[0, g, side, p]
+        enter_less(g, taken[1], lambda p: come[1, g, taken[1], p])
+
+    def merge_cross(k):
+        g = straight[0] + k
+        for side in range(2):
+            best = [own[0, g, side, p] for p in range(packs)]
+            for i in range(SIDE - 1):
+                take = key_of(come_x[i, k, side, packs - 1]) > key_of(best[-1])
+                best = [jnp.where(take, come_x[i, k, side, p], best[p]) for p in range(packs)]
             for p in range(packs):
-                enter[g, side, p] = come[0, g, side, p]
-                enter[g, 1 - side, p] = jnp.where(key_rows, NONE if p == packs - 1 else 0.0, 0.0)
-        else:
-            take = key_of(come[stage, g, side, packs - 1]) > key_of(enter[g, side, packs - 1])
+                own[2, g, side, p] = best[p]
+
+    def note_cross(k):
+        g = straight[0] + k
+        for side in range(2):
+            clear(g, side)
+        for i in range(SIDE - 1):
+            enter_less(g, cross_takes[i], lambda p: come_x[i, k, cross_takes[i], p])
+
+    def note_rows(g):
+        for d in range(SIDE - 1):
+            enter_less(g, row_takes[d], lambda p: come_y[g, d, p])
+
+    def turn_along(k):
+        g = turned[0] + k
+        for side in range(2):
+            clear(g, side)
+        note_rows(g)
+        for side in range(2):
+            take = key_of(own[0, g, side, packs - 1]) > key_of(enter[g, side, packs - 1])
             for p in range(packs):
-                enter[g, side, p] = jnp.where(take, come[stage, g, side, p], enter[g, side, p])
+                before = enter[g, side, p]
+                own[2 - side, g, side, p] = jnp.where(take, own[0, g, side, p], before)
+                own[1 + side, g, side, p] = before
+
+    def complete_rows(g):
+        note_rows(g)
+        complete(g)
+
+    def complete_turned(k):
+        g = turned[0] + k
+        for i in range(SIDE - 1):
+            for side in range(2):
+                enter_less(g, side, lambda p: come_x[i, straight[1] + k, side, p])
+        complete(g)
 
     def complete(g):
-        for d in range(SIDE - 1):
-            side = row_takes[d]
-            take = key_of(come_y[g, d, packs - 1]) > key_of(enter[g, side, packs - 1])
-            for p in range(packs):
-                enter[g, side, p] = jnp.where(take, come_y[g, d, p], enter[g, side, p])
         has = [key_of(enter[g, s, packs - 1]) > NONE for s in range(2)]
         mine = [key_of(own[0, g, s, packs - 1]) > NONE for s in range(2)]
         for p in range(packs):
@@ -232,39 +335,77 @@
                 out_ref[b, :, cols] = f + weight * (n - f)
 
     loaded = 0
-    for m, (start, count) in enumerate(messages):
+
+    def summarize_part(start, count):
+        nonlocal loaded
         while loaded < len(loads) and loads[loaded][0] < start + count:
             load_v(loaded).wait()
             load_x(loaded).wait()
             loaded += 1
-        over(m, summarize)
+        over(start, count, summarize)
+
+    summarized = set()
+    for m, (start, count, _, _) in enumerate(messages):
+        if m == min(MIDDLE, len(messages) - 1):
+            cross(0, 2).start()
+        if start not in summarized:
+            summarize_part(start, count)
+            summarized.add(start)
         if m == 0:
-            pl.semaphore_wait(barrier, len(pair) + len(rows))
+            pl.semaphore_wait(barrier, len(pair) + len(rows) + 1)
         swap(0, m).start()
-
-    for stage, m in arrival_order(messages):
-        if stage < 2:
-            swap(stage, m).wait_recv()
-            over(m, functools.partial(merge_pair, stage))
-            if stage == 0:
-                swap(1, m).start()
+        if m == min(EARLY, len(messages) - 1) - 1 or len(messages) == 1:
+            summarize_part(*turned)
+            for d in range(SIDE - 1):
+                to_row(d, len(row_parts) - 1).start()
+            summarize_part(*straight)
+            cross(0, 0).start()
+            cross(0, 1).start()
+
+    for kind, i in order:
+        if kind < 2:
+            start, count, side, sides = messages[i]
+            swap(kind, i).wait_recv()
+            over(start, count, functools.partial(merge_pair, kind, range(side, side + sides)))
+            if kind == 0:
+                swap(1, i).start()
             else:
                 for d in range(SIDE - 1):
-                    to_row(d, m).start()
-            over(m, functools.partial(note_pair, stage))
+                    if sides == 2:
+                        to_row(d, owner[i]).start()
+                    else:
+                        pl.when(row_gives[d] == side)(to_row(d, owner[i]).start)
+                if side + sides == 2:
+                    over(start, count, note_pair)
+        elif kind == 2:
+            crossed(come_x.at[:, places[0]], 0).wait_recv()
+            over(0, straight[1], merge_cross)
+            for d in range(SIDE - 1):
+                to_row(d, len(row_parts) - 2).start()
+            over(0, straight[1], note_cross)
+        elif kind == 3:
+            from_rows(pl.ds(*row_parts[i]), i).wait_recv()
+            over(*row_parts[i], complete_rows)
+        elif kind == 4:
+            from_rows(pl.ds(*turned), len(row_parts) - 1).wait_recv()
+            over(0, turned[1], turn_along)
+            for k in range(SIDE - 1):
+                cross(1, k).start()
         else:
-            from_rows(pl.ds(*messages[m]), m).wait_recv()
-            over(m, complete)
+            crossed(come_x.at[:, places[1]], 1).wait_recv()
+            over(0, turned[1], complete_turned)
 
     for stage in range(2):
+        part = pl.ds(0, straight[0])
         pltpu.make_async_remote_copy(
-            src_ref=own.at[stage],
-            dst_ref=come.at[stage],
+            src_ref=own.at[stage, part],
+            dst_ref=come.at[stage, part],
             send_sem=send_sem.at[stage],
-            recv_sem=recv_sem.at[stage, 0],
+            recv_sem=recv_sem.at[0],
             device_id=pair[stage],
             device_id_type=MESH,
         ).wait_send()
+    crossed(come_x, 0).wait_send()
     from_rows(pl.ds(0, groups), 0).wait_send()
 
 
@@ -272,7 +413,8 @@
     dates, bands, pixels = reflectance.shape
     groups = pixels // (TILES * LANES)
     packs = (bands + 1) // 2
-    messages, loads = len(spans(SHARES, groups)), len(spans(LOADS, groups))
+    messages, _, rows, _ = plan(groups)
+    loads = len(pieces(LOADS, groups))
     hbm = pl.BlockSpec(memory_space=pltpu.HBM)
     filled = pl.pallas_call(
         functools.partial(scan_fill, bands, groups),
@@ -285,13 +427,14 @@
             pltpu.VMEM((dates, pixels), jnp.int32),
             pltpu.VMEM((3, groups, 2, packs, ROWS, LANES), jnp.float32),
             pltpu.VMEM((2, groups, 2, packs, ROWS, LANES), jnp.float32),
+            pltpu.VMEM((SIDE - 1, rows[-2][1] + rows[-1][1], 2, packs, ROWS, LANES), jnp.float32),
             pltpu.VMEM((groups, SIDE - 1, packs, ROWS, LANES), jnp.float32),
             pltpu.VMEM((groups, 2, packs, ROWS, LANES), jnp.float32),
             pltpu.SemaphoreType.DMA,
             pltpu.SemaphoreType.DMA((loads,)),
             pltpu.SemaphoreType.DMA((loads,)),
-            pltpu.SemaphoreType.DMA((3,)),
-            pltpu.SemaphoreType.DMA((3, messages)),
+            pltpu.SemaphoreType.DMA((4,)),
+            pltpu.SemaphoreType.DMA((2 * len(messages) + 2 + len(rows),)),
         ],
         compiler_params=pltpu.CompilerParams(
             collective_id=0, has_side_effects=True, vmem_limit_bytes=(62 << 20) - 65536

time: 26.8 us -> 26.1 us (0.974)
  Pallas kernels: 25.4 us -> 24.8 us
    pallas_call x1, Pallas kernels: 25.4 us -> 24.8 us  [body(): pl.pallas_call(functools.partial(scan_fill, bands, groups), out_shape=plt...]
where the time goes in v4:
time: 26.1 us; the launch traced here: 26 us
  Pallas kernels  24.8 us (95%)
  local copies, waits for them, and re-layouts  1.23 us (5%)
    pallas_call x1, Pallas kernels, body(): pl.pallas_call(functools.partial(scan_fill, bands, groups), out_shape=plt...  24.8 us
    unnamed x1, local copies, waits for them, and re-layouts  1.23 us

profile of v4, /device:TPU:0, one launch (start us, length us, event | category | flops | bytes accessed | tf_op | source)
XLA Modules:
  0.0 26.0 jit_solution(9451810817123157830)
XLA Ops:
  0.0 24.8 %scan_fill.1 = f32[7,8,8192]{2,1,0:T(8,128)S(1)} custom-call(s32[8]{0:T(128)} %days_hbm.1, f32[7,8,8192]{2,1,0:T(8,128)} %bitcast.3, s32[8,8192]{1,0:T(8,128)} %v_hbm.1), custom_call_target="tpu_custom_call" | custom-call | tf_op jit(solution)/shard_map/scan_fill/pallas_call | solution.py:419
  24.8 1.2 %copy.5 = f32[8,7,8192]{2,0,1:T(8,128)} copy(f32[8,7,8192]{2,0,1:T(8,128)S(1)} %bitcast.2) | data formatting | bytes 3670016

commit v5 on v4

--- a/solution.py
+++ b/solution.py
@@ -13,13 +13,14 @@
 LANES = 128
 ROWS = 8
 TILES = 4
+FAR_FIRST = (1, 0, 2)
 SIDE = 4
 NONE = -1073741824.0
 STRAIGHT, TURNED = 1, 2
-SHARES = (-1, 1, 2, 2, 2, 2, 1, 1, -1)
+SHARES = (-1, 1, 2, 2, 2, 2, 1, -1, -1)
 LOADS = (2, 6, 8)
 UNIT, HOP, FAR = 0.35, 3.0, 4.0
-EARLY, MIDDLE = 5, 10
+EARLY, MIDDLE = 5, 11
 TURN = 16
 
 
@@ -370,7 +371,7 @@
             if kind == 0:
                 swap(1, i).start()
             else:
-                for d in range(SIDE - 1):
+                for d in FAR_FIRST:
                     if sides == 2:
                         to_row(d, owner[i]).start()
                     else:
@@ -380,7 +381,7 @@
         elif kind == 2:
             crossed(come_x.at[:, places[0]], 0).wait_recv()
             over(0, straight[1], merge_cross)
-            for d in range(SIDE - 1):
+            for d in FAR_FIRST:
                 to_row(d, len(row_parts) - 2).start()
             over(0, straight[1], note_cross)
         elif kind == 3:

time: 26.1 us -> 26.1 us (level)
  no operation moved by 1% of the time
where the time goes in v5:
time: 26.1 us; the launch traced here: 26 us
  Pallas kernels  24.7 us (95%)
  local copies, waits for them, and re-layouts  1.23 us (5%)
    pallas_call x1, Pallas kernels, body(): pl.pallas_call(functools.partial(scan_fill, bands, groups), out_shape=plt...  24.7 us
    unnamed x1, local copies, waits for them, and re-layouts  1.23 us

profile of v5, /device:TPU:0, one launch (start us, length us, event | category | flops | bytes accessed | tf_op | source)
XLA Modules:
  0.0 26.0 jit_solution(3824468989259270269)
XLA Ops:
  0.0 24.7 %scan_fill.1 = f32[7,8,8192]{2,1,0:T(8,128)S(1)} custom-call(s32[8]{0:T(128)} %days_hbm.1, f32[7,8,8192]{2,1,0:T(8,128)} %bitcast.3, s32[8,8192]{1,0:T(8,128)} %v_hbm.1), custom_call_target="tpu_custom_call" | custom-call | tf_op jit(solution)/shard_map/scan_fill/pallas_call | solution.py:420
  24.7 1.2 %copy.5 = f32[8,7,8192]{2,0,1:T(8,128)} copy(f32[8,7,8192]{2,0,1:T(8,128)S(1)} %bitcast.2) | data formatting | bytes 3670016

commit v6 on v5

--- a/solution.py
+++ b/solution.py
@@ -18,7 +18,7 @@
 NONE = -1073741824.0
 STRAIGHT, TURNED = 1, 2
 SHARES = (-1, 1, 2, 2, 2, 2, 1, -1, -1)
-LOADS = (2, 6, 8)
+LOADS = (2, 14)
 UNIT, HOP, FAR = 0.35, 3.0, 4.0
 EARLY, MIDDLE = 5, 11
 TURN = 16

time: 26.1 us -> 26.1 us (level)
  no operation moved by 1% of the time
where the time goes in v6:
time: 26.1 us; the launch traced here: 26 us
  Pallas kernels  24.7 us (95%)
  local copies, waits for them, and re-layouts  1.23 us (5%)
    pallas_call x1, Pallas kernels, body(): pl.pallas_call(functools.partial(scan_fill, bands, groups), out_shape=plt...  24.7 us
    unnamed x1, local copies, waits for them, and re-layouts  1.23 us

profile of v6, /device:TPU:0, one launch (start us, length us, event | category | flops | bytes accessed | tf_op | source)
XLA Modules:
  0.0 26.0 jit_solution(3888251231250634980)
XLA Ops:
  0.0 24.7 %scan_fill.1 = f32[7,8,8192]{2,1,0:T(8,128)S(1)} custom-call(s32[8]{0:T(128)} %days_hbm.1, f32[7,8,8192]{2,1,0:T(8,128)} %bitcast.3, s32[8,8192]{1,0:T(8,128)} %v_hbm.1), custom_call_target="tpu_custom_call" | custom-call | tf_op jit(solution)/shard_map/scan_fill/pallas_call | solution.py:420
  24.7 1.2 %copy.5 = f32[8,7,8192]{2,0,1:T(8,128)} copy(f32[8,7,8192]{2,0,1:T(8,128)S(1)} %bitcast.2) | data formatting | bytes 3670016
